TPU v7x, 128 devices: a whole 4x4x4 slice. The times are simulated.
128 devices in a mesh: gx: 4 (over z_lo, core), gy: 8 (over z_hi, y), gz: 4 (over x).
Axes of the slice: x: 4, y: 4, z: 4 (z_hi: 2, z_lo: 2; z = z_hi * 2 + z_lo), core: 2. Of those that a mesh axis runs over, the one named last changes fastest.
Arguments:
- cell_volume: float32 [64, 128, 512], P('gx', 'gy', 'gz'), may hold values from 0.5 to 2
- exponent: int32 [64, 128, 512], P('gx', 'gy', 'gz'), may hold values from 0 to 7
- owner_row: int32 [32768], P(('gx', 'gy', 'gz')), may hold values from 0 to 32767, as said below
Outputs:
- stencil_out: float32 [27, 32768, 128], P(None, ('gx', 'gy', 'gz'))
- lumped_out: float32 [32768, 128], P(('gx', 'gy', 'gz'))
Inputs may be any that keep to these rules, and one draw needn't show every extreme that they name: owner_row is a permutation of the row blocks; the row blocks of each device's share of owner_row go to each owner (owner_row // 256) exactly 2 times.
All inputs are finite; a program needn't handle non-finite values.
Results may differ from a plain program's by a relative error of at most 0.00007.
Values sent between devices are 32-bit elements; how exact they have to be, the bound alone decides.
A program may use at most 64 MiB of HBM per device.

v0:
```python
import jax
import jax.numpy as jnp
import numpy as np
from jax import lax
from jax.sharding import PartitionSpec as P

log_step = 0.3


def from_behind(block, axis, distance):
    devices = range(lax.axis_size(axis))
    route = [((i - distance) % len(devices), i) for i in devices]
    return lax.ppermute(block, axis, route)


def weight_table():
    table = np.zeros((27, 8), np.float32)
    for index_o in range(27):
        offsets = (index_o // 9 - 1, index_o // 3 % 3 - 1, index_o % 3 - 1)
        for index_a in range(8):
            corner = (index_a // 4, index_a // 2 % 2, index_a % 2)
            inside = all((0 <= corner[slot_d] + offsets[slot_d] <= 1 for slot_d in range(3)))
            factor = 1.0
            for slot_d in range(3):
                factor = factor * (2.0 if offsets[slot_d] == 0 else 1.0)
            table[index_o, index_a] = factor / 64.0 if inside else 0.0
    return table


def rim_section(current, along, stack_at, sender):
    length = current.shape[along]
    interior = lax.slice_in_dim(current, 0, length - 1, axis=along)
    top_layer = lax.slice_in_dim(current, length - 1, length, axis=along)
    received = sender(top_layer)
    behind = jnp.concatenate([received, interior], axis=along)
    return jnp.stack([current, behind], axis=stack_at)


def shards(cell_volume, exponent, owner_row):
    weight = cell_volume * jnp.exp(-log_step * exponent.astype(jnp.float32))
    span_x, span_y, span_z = weight.shape
    line_count = span_x * span_y
    devices_all = lax.axis_size(("gx", "gy", "gz"))

    def send_z(rim_layer):
        return from_behind(rim_layer, "gz", 1)

    def send_x(rim_layer):
        return from_behind(rim_layer, "gx", 1)

    def send_y(rim_layer):
        return from_behind(rim_layer, "gy", 1)

    owner_dev = owner_row // line_count
    by_owner = jnp.argsort(owner_dev, stable=True)
    slot_ids = (owner_row % line_count)[by_owner].reshape(1, devices_all, -1)
    table = jnp.asarray(weight_table())
    sectioned_z = rim_section(weight, 2, 0, send_z)
    sectioned_x = rim_section(sectioned_z, 1, 0, send_x)
    sectioned_all = rim_section(sectioned_x, 3, 1, send_y)
    corners = sectioned_all.reshape(8, line_count, span_z)
    packed = corners[:, by_owner].reshape(8, devices_all, -1, span_z)
    got_rows, got_slots = (
        lax.all_to_all(packed, ("gx", "gy", "gz"), split_axis=1, concat_axis=1, tiled=True),
        lax.all_to_all(slot_ids, ("gx", "gy", "gz"), split_axis=1, concat_axis=1, tiled=True),
    )
    placing = jnp.argsort(got_slots.reshape(-1))
    placed = got_rows.reshape(8, line_count, span_z)[:, placing]
    stencil_rows = jnp.einsum("oa,alz->olz", table, placed, precision=lax.Precision.HIGHEST)
    lumped_rows = 1.0 / jnp.sum(stencil_rows, axis=0)
    return (stencil_rows, lumped_rows)


def solution(mesh):
    return jax.shard_map(
        shards,
        mesh=mesh,
        in_specs=(P("gx", "gy", "gz"), P("gx", "gy", "gz"), P(("gx", "gy", "gz"))),
        out_specs=(P(None, ("gx", "gy", "gz"), None), P(("gx", "gy", "gz"), None)),
        check_vma=False,
    )
```

profile of v0, /device:TPU:1, one launch (start us, length us, event | category | flops | bytes accessed | tf_op | source)
XLA Modules:
  0.0 70.4 jit_solution(13474387986052149990)
XLA Ops:
  0.6 1.0 %exponential_multiply_fusion = f32[16,16,128]{2,1,0:T(8,128)S(1)} fusion(f32[16,16,128]{2,1,0:T(8,128)} %param.4, s32[16,16,128]{2,1,0:T(8,128)} %param.5), kind=kLoop, calls=%fused_computation.23 | loop fusion | flops 98304 | bytes 393216 | tf_op jit(solution)/shard_map/mul | solution.py:40
  1.7 2.1 %collective-permute-start = (f32[16,16,1]{2,1,0:T(8,128)S(1)}, f32[16,16,1]{2,1,0:T(8,128)S(1)}, u32[]{:S(2)}, u32[]{:S(2)}) collective-permute-start(f32[16,16,1]{2,1,0:T(8,128)S(1)} %slice.30), channel_id=1, source_target_pairs={{3,0},{0,1},{1,2},{2,3},{7,4},{4,5},{5,6},{6,7},{11,8},{8,9},{9,10... | collective-permute-start | bytes 3080 | tf_op jit(solution)/shard_map/ppermute | solution.py:13
  3.8 0.7 and_select_fusion
  4.5 3.2 %sort.34 = (s32[256]{0:T(256)}, s32[256]{0:T(256)S(1)}) sort(s32[256]{0:T(256)S(1)} %get-tuple-element.13, s32[256]{0:T(256)S(1)} %iota.8), dimensions={0}, to_apply=%region_0.1 | sort | flops 2048 | bytes 4096 | tf_op jit(solution)/shard_map/jit(argsort)/sort | solution.py:55
  7.7 1.9 %gather_fusion.1 = s32[256]{0:T(256)S(1)} fusion(s32[256]{0:T(256)S(1)} %get-tuple-element.12, s32[1024]{0:T(1024)S(1)} %pad_clamp_fusion.1), kind=kCustom, calls=%fused_computation.1 | custom fusion | bytes 3072 | tf_op jit(solution)/shard_map/gather | solution.py:56
  9.6 0.8 %reshape.22 = s32[1,128,2]{2,1,0:T(8,128)} reshape(s32[256]{0:T(256)S(1)} %gather_fusion.1) | data formatting | bytes 2048 | tf_op jit(solution)/shard_map/reshape | solution.py:56
  10.4 10.7 %all-to-all-start.1 = ((s32[1,128,2]{2,0,1:T(1,128)}), s32[1,128,2]{2,0,1:T(1,128)S(1)}, u32[]{:S(2)}, u32[]{:S(2)}) async-start(s32[1,128,2]{2,0,1:T(1,128)} %bitcast.12), calls=%async_computation.1 | async-start | bytes 131072 | tf_op jit(solution)/shard_map/all_to_all | solution.py:65
  21.1 0.1 maximum_bitcast_fusion.2
  21.2 1.8 %collective-permute-start.1 = (f32[2,1,16,128]{3,2,1,0:T(8,128)S(1)}, f32[2,1,16,128]{3,2,1,0:T(8,128)S(1)}, u32[]{:S(2)}, u32[]{:S(2)}) collective-permute-start(f32[2,1,16,128]{3,2,1,0:T(8,128)S(1)} %fusion.7), channel_id=1, source_target_pairs={{96,0},{0,32},{32,64},{64,96},{97,1},{1,33},{33,65},{65,97},{98,2}... | collective-permute-start | bytes 49160 | tf_op jit(solution)/shard_map/ppermute | solution.py:13
  23.1 0.8 %collective-permute-done.1 = f32[2,1,16,128]{3,2,1,0:T(8,128)S(1)} collective-permute-done((f32[2,1,16,128]{3,2,1,0:T(8,128)S(1)}, f32[2,1,16,128]{3,2,1,0:T(8,128)S(1)}, u32[]{:S(2)}, u32[]{:S(2)}) %collective-permute-start.1) | collective-permute-done | bytes 16416 | tf_op jit(solution)/shard_map/ppermute | solution.py:13
  24.0 1.3 %collective-permute-start.2 = (f32[2,2,16,1,128]{4,3,2,1,0:T(1,128)S(1)}, f32[2,2,16,1,128]{4,3,2,1,0:T(1,128)S(1)}, u32[]{:S(2)}, u32[]{:S(2)}) collective-permute-start(f32[2,2,16,1,128]{4,3,2,1,0:T(1,128)S(1)} %fusion.6), channel_id=1, source_target_pairs={{28,0},{0,4},{4,8},{8,12},{12,16},{16,20},{20,24},{24,28},{29,1},{... | collective-permute-start | bytes 98312 | tf_op jit(solution)/shard_map/ppermute | solution.py:13
  25.4 5.6 %collective-permute-done.2 = f32[2,2,16,1,128]{4,3,2,1,0:T(1,128)S(1)} collective-permute-done((f32[2,2,16,1,128]{4,3,2,1,0:T(1,128)S(1)}, f32[2,2,16,1,128]{4,3,2,1,0:T(1,128)S(1)}, u32[]{:S(2)}, u32[]{:S(2)}) %collective-permute-start.2) | collective-permute-done | bytes 32800 | tf_op jit(solution)/shard_map/ppermute | solution.py:13
  31.1 0.6 copy.11
  31.7 2.0 %gather_fusion = f32[256,8,128]{2,1,0:T(8,128)} fusion(f32[8,256,128]{2,0,1:T(8,128)S(1)} %copy.11, s32[1024]{0:T(1024)S(1)} %pad_clamp_fusion.1), kind=kCustom, calls=%fused_computation | custom fusion | bytes 2098176 | tf_op jit(solution)/shard_map/gather | solution.py:62
  33.7 8.5 %all-to-all-start = ((f32[8,128,2,128]{3,0,2,1:T(8,128)}), f32[8,128,2,128]{3,0,2,1:T(8,128)S(1)}, u32[]{:S(2)}, u32[]{:S(2)}) async-start(f32[8,128,2,128]{3,0,2,1:T(8,128)} %bitcast.10), calls=%async_computation | async-start | bytes 2097152 | tf_op jit(solution)/shard_map/all_to_all | solution.py:64
  42.2 0.5 broadcast.50
  42.7 0.8 %reduce.3 = s32[128,2]{1,0:T(8,128)S(1)} reduce(s32[1,128,2]{2,0,1:T(1,128)S(1)} %all-to-all-done.1, s32[]{:T(128)} %broadcast.50), dimensions={0}, to_apply=%all_to_all.7.reduce_sub_computation.3 | reduce | bytes 2052 | tf_op jit(solution)/shard_map/all_to_all | solution.py:65
  43.6 0.1 reshape.23
  43.7 3.2 %sort.35 = (s32[256]{0:T(256)}, s32[256]{0:T(256)S(1)}) sort(s32[256]{0:T(256)S(1)} %reshape.23, s32[256]{0:T(256)S(1)} %iota.9), dimensions={0}, to_apply=%region_1.2 | sort | flops 2048 | bytes 4096 | tf_op jit(solution)/shard_map/jit(argsort)/sort | solution.py:67
  46.9 14.2 %all-to-all-done = f32[8,128,2,128]{3,0,2,1:T(8,128)S(1)} async-done(((f32[8,128,2,128]{3,0,2,1:T(8,128)}), f32[8,128,2,128]{3,0,2,1:T(8,128)S(1)}, u32[]{:S(2)}, u32[]{:S(2)}) %all-to-all-start) | async-done | bytes 1048608 | tf_op jit(solution)/shard_map/all_to_all | solution.py:64
  61.1 1.0 %gather_fusion.2 = f32[256,8,128]{2,1,0:T(8,128)S(1)} fusion(f32[8,256,128]{2,0,1:T(8,128)S(1)} %bitcast.33, s32[1024]{0:T(1024)S(1)} %pad_clamp_fusion), kind=kCustom, calls=%fused_computation.2 | custom fusion | bytes 2098176 | tf_op jit(solution)/shard_map/gather | solution.py:68
  62.1 3.7 %fusion.8 = (f32[256,128]{1,0:T(8,128)S(1)}, f32[27,256,128]{2,0,1:T(8,128)S(1)}) fusion(f32[27,8,1]{0,1,2:T(8,128)S(1)} %copy-done, f32[256,8,128]{2,1,0:T(8,128)S(1)} %gather_fusion.2), kind=kOutput, calls=%fused_computation.38 | convolution fusion | flops 85786624 | bytes 4719456 | tf_op jit(solution)/shard_map/oa,alz->olz/dot_general | solution.py:69
  65.9 0.7 broadcast_divide_fusion
  66.5 3.8 %copy.13 = f32[27,256,128]{2,1,0:T(8,128)} copy(f32[27,256,128]{2,0,1:T(8,128)S(1)} %get-tuple-element.15) | data formatting | bytes 7077888
  (20 shorter events, 0.4 us)
Async XLA Ops:
  1.7 19.4 %collective-permute-start = (f32[16,16,1]{2,1,0:T(8,128)S(1)}, f32[16,16,1]{2,1,0:T(8,128)S(1)}, u32[]{:S(2)}, u32[]{:S(2)}) collective-permute-start(f32[16,16,1]{2,1,0:T(8,128)S(1)} %slice.30), channel_id=1, source_target_pairs={{3,0},{0,1},{1,2},{2,3},{7,4},{4,5},{5,6},{6,7},{11,8},{8,9},{9,10... | collective-permute-start | bytes 3080 | tf_op jit(solution)/shard_map/ppermute | solution.py:13
  10.4 23.3 %all-to-all-start.1 = ((s32[1,128,2]{2,0,1:T(1,128)}), s32[1,128,2]{2,0,1:T(1,128)S(1)}, u32[]{:S(2)}, u32[]{:S(2)}) async-start(s32[1,128,2]{2,0,1:T(1,128)} %bitcast.12), calls=%async_computation.1 | async-start | bytes 131072 | tf_op jit(solution)/shard_map/all_to_all | solution.py:65
  21.2 2.7 %collective-permute-start.1 = (f32[2,1,16,128]{3,2,1,0:T(8,128)S(1)}, f32[2,1,16,128]{3,2,1,0:T(8,128)S(1)}, u32[]{:S(2)}, u32[]{:S(2)}) collective-permute-start(f32[2,1,16,128]{3,2,1,0:T(8,128)S(1)} %fusion.7), channel_id=1, source_target_pairs={{96,0},{0,32},{32,64},{64,96},{97,1},{1,33},{33,65},{65,97},{98,2}... | collective-permute-start | bytes 49160 | tf_op jit(solution)/shard_map/ppermute | solution.py:13
  24.0 6.9 %collective-permute-start.2 = (f32[2,2,16,1,128]{4,3,2,1,0:T(1,128)S(1)}, f32[2,2,16,1,128]{4,3,2,1,0:T(1,128)S(1)}, u32[]{:S(2)}, u32[]{:S(2)}) collective-permute-start(f32[2,2,16,1,128]{4,3,2,1,0:T(1,128)S(1)} %fusion.6), channel_id=1, source_target_pairs={{28,0},{0,4},{4,8},{8,12},{12,16},{16,20},{20,24},{24,28},{29,1},{... | collective-permute-start | bytes 98312 | tf_op jit(solution)/shard_map/ppermute | solution.py:13
  31.1 31.0 %copy-start = (f32[27,8,1]{0,1,2:T(8,128)S(1)}, f32[27,8,1]{0,1,2:T(8,128)}, u32[]{:S(2)}) copy-start(f32[27,8,1]{0,1,2:T(8,128)} %constant.39) | copy-start | bytes 2596
  33.7 27.3 %all-to-all-start = ((f32[8,128,2,128]{3,0,2,1:T(8,128)}), f32[8,128,2,128]{3,0,2,1:T(8,128)S(1)}, u32[]{:S(2)}, u32[]{:S(2)}) async-start(f32[8,128,2,128]{3,0,2,1:T(8,128)} %bitcast.10), calls=%async_computation | async-start | bytes 2097152 | tf_op jit(solution)/shard_map/all_to_all | solution.py:64
where the time goes:
time: 70.6 us; the launch traced here: 70.4 us
  starting transfers between devices  24.4 us (35%)
  waiting for transfers between devices  20.6 us (29%)
  local copies, waits for them, and re-layouts  10.9 us (15%)
  other arithmetic  9.93 us (14%)
  matrix products  3.73 us (5%)
  between operations  0.8 us (1%)
    all_to_all x1, waiting for transfers between devices, shards(): lax.all_to_all(packed, ('gx', 'gy', 'gz'), split_axis=1, concat_axis=1, t...  14.2 us
    all_to_all x1, starting transfers between devices, shards(): lax.all_to_all(slot_ids, ('gx', 'gy', 'gz'), split_axis=1, concat_axis=1,...  10.7 us
    all_to_all x1, starting transfers between devices, shards(): lax.all_to_all(packed, ('gx', 'gy', 'gz'), split_axis=1, concat_axis=1, t...  8.48 us
    ppermute x3, waiting for transfers between devices, from_behind(): return lax.ppermute(block, axis, route)  6.43 us
    ppermute x3, starting transfers between devices, from_behind(): return lax.ppermute(block, axis, route)  5.24 us
    unnamed x3, local copies, waits for them, and re-layouts  3.85 us
    dot_general x1, matrix products, shards(): jnp.einsum('oa,alz->olz', table, placed, precision=lax.Precision.HIGHEST)  3.73 us
    sort x1, other arithmetic, shards(): by_owner = jnp.argsort(owner_dev, stable=True)  3.17 us
  transfers between devices with their start and end apart: 5, of which 3 were waited for; matrix products, arithmetic and copies ran while one was open for 20% of the time, Pallas kernels for 0%

commit v1 on v0

--- a/solution.py
+++ b/solution.py
@@ -5,6 +5,13 @@
 from jax.sharding import PartitionSpec as P
 
 log_step = 0.3
+
+
+def swap_blocks(array, mesh_axis, split, join):
+    n_dev = lax.axis_size(mesh_axis)
+    parts = jnp.stack(jnp.split(array, n_dev, axis=split), axis=0)
+    parts = lax.all_to_all(parts, mesh_axis, split_axis=0, concat_axis=0)
+    return jnp.concatenate(parts, axis=join)
 
 
 def from_behind(block, axis, distance):
@@ -61,7 +68,7 @@
     corners = sectioned_all.reshape(8, line_count, span_z)
     packed = corners[:, by_owner].reshape(8, devices_all, -1, span_z)
     got_rows, got_slots = (
-        lax.all_to_all(packed, ("gx", "gy", "gz"), split_axis=1, concat_axis=1, tiled=True),
+        swap_blocks(packed, ("gx", "gy", "gz"), 1, 1),
         lax.all_to_all(slot_ids, ("gx", "gy", "gz"), split_axis=1, concat_axis=1, tiled=True),
     )
     placing = jnp.argsort(got_slots.reshape(-1))

time: 70.6 us -> 146 us (2.07)
  local copies, waits for them, and re-layouts: 10.9 us -> 86.6 us
    unnamed x3 -> x130, local copies, waits for them, and re-layouts: 3.85 us -> 79.9 us
  transfers between devices with their start and end apart: 5 -> 5, of which waited for: 3 -> 3; matrix products, arithmetic and copies ran while one was open for 20% -> 62% of each run, Pallas kernels for 0% -> 0%
where the time goes in v1:
time: 146 us
  local copies, waits for them, and re-layouts  86.6 us (59%)
  starting transfers between devices  24.4 us (17%)
  waiting for transfers between devices  20.6 us (14%)
  other arithmetic  9.93 us (7%)
  matrix products  3.72 us (3%)
    unnamed x130, local copies, waits for them, and re-layouts  79.9 us
    all_to_all x1, waiting for transfers between devices, swap_blocks(): parts = lax.all_to_all(parts, mesh_axis, split_axis=0, concat_axis=0)  14.2 us
    all_to_all x1, starting transfers between devices, shards(): lax.all_to_all(slot_ids, ('gx', 'gy', 'gz'), split_axis=1, concat_axis=1,...  10.7 us
    all_to_all x1, starting transfers between devices, swap_blocks(): parts = lax.all_to_all(parts, mesh_axis, split_axis=0, concat_axis=0)  8.49 us
    ppermute x3, waiting for transfers between devices, from_behind(): return lax.ppermute(block, axis, route)  6.43 us
    ppermute x3, starting transfers between devices, from_behind(): return lax.ppermute(block, axis, route)  5.24 us
    dot_general x1, matrix products, shards(): jnp.einsum('oa,alz->olz', table, placed, precision=lax.Precision.HIGHEST)  3.72 us
    sort x1, other arithmetic, shards(): by_owner = jnp.argsort(owner_dev, stable=True)  3.17 us
  transfers between devices with their start and end apart: 5, of which 3 were waited for; matrix products, arithmetic and copies ran while one was open for 62% of the time, Pallas kernels for 0%

profile of v1, /device:TPU:1, one launch (start us, length us, event | category | flops | bytes accessed | tf_op | source)
XLA Modules:
  0.0 146.1 jit_solution(7556392448466282280)
XLA Ops:
  0.6 1.0 exponential_multiply_fusion
  1.7 2.1 %collective-permute-start = (f32[16,16,1]{2,1,0:T(8,128)S(1)}, f32[16,16,1]{2,1,0:T(8,128)S(1)}, u32[]{:S(2)}, u32[]{:S(2)}) collective-permute-start(f32[16,16,1]{2,1,0:T(8,128)S(1)} %slice.30), channel_id=1, source_target_pairs={{3,0},{0,1},{1,2},{2,3},{7,4},{4,5},{5,6},{6,7},{11,8},{8,9},{9,10... | collective-permute-start | bytes 3080 | tf_op jit(solution)/shard_map/ppermute | solution.py:20
  3.8 0.7 and_select_fusion
  4.5 3.2 %sort.34 = (s32[256]{0:T(256)}, s32[256]{0:T(256)S(1)}) sort(s32[256]{0:T(256)S(1)} %get-tuple-element.13, s32[256]{0:T(256)S(1)} %iota.8), dimensions={0}, to_apply=%region_0.1 | sort | flops 2048 | bytes 4096 | tf_op jit(solution)/shard_map/jit(argsort)/sort | solution.py:62
  7.7 1.9 %gather_fusion.1 = s32[256]{0:T(256)S(1)} fusion(s32[256]{0:T(256)S(1)} %get-tuple-element.12, s32[1024]{0:T(1024)S(1)} %pad_clamp_fusion.1), kind=kCustom, calls=%fused_computation.1 | custom fusion | bytes 3072 | tf_op jit(solution)/shard_map/gather | solution.py:63
  9.6 0.8 reshape.22
  10.4 10.7 %all-to-all-start.1 = ((s32[1,128,2]{2,0,1:T(1,128)}), s32[1,128,2]{2,0,1:T(1,128)S(1)}, u32[]{:S(2)}, u32[]{:S(2)}) async-start(s32[1,128,2]{2,0,1:T(1,128)} %bitcast.143), calls=%async_computation.1 | async-start | bytes 131072 | tf_op jit(solution)/shard_map/all_to_all | solution.py:72
  21.2 1.8 %collective-permute-start.1 = (f32[2,1,16,128]{3,2,1,0:T(8,128)S(1)}, f32[2,1,16,128]{3,2,1,0:T(8,128)S(1)}, u32[]{:S(2)}, u32[]{:S(2)}) collective-permute-start(f32[2,1,16,128]{3,2,1,0:T(8,128)S(1)} %fusion.7), channel_id=1, source_target_pairs={{96,0},{0,32},{32,64},{64,96},{97,1},{1,33},{33,65},{65,97},{98,2}... | collective-permute-start | bytes 49160 | tf_op jit(solution)/shard_map/ppermute | solution.py:20
  23.1 0.8 collective-permute-done.1
  24.0 1.3 collective-permute-start.2
  25.4 5.6 %collective-permute-done.2 = f32[2,2,16,1,128]{4,3,2,1,0:T(1,128)S(1)} collective-permute-done((f32[2,2,16,1,128]{4,3,2,1,0:T(1,128)S(1)}, f32[2,2,16,1,128]{4,3,2,1,0:T(1,128)S(1)}, u32[]{:S(2)}, u32[]{:S(2)}) %collective-permute-start.2) | collective-permute-done | bytes 32800 | tf_op jit(solution)/shard_map/ppermute | solution.py:20
  31.1 0.6 copy.265
  31.7 1.0 gather_fusion
  32.8 0.6 constant_dynamic-update-slice_fusion.127
  33.4 0.6 constant_dynamic-update-slice_fusion.126
  34.0 0.6 constant_dynamic-update-slice_fusion.125
  109.5 8.5 %all-to-all-start = ((f32[128,8,1,2,128]{4,1,3,2,0:T(8,128)}), f32[128,8,1,2,128]{4,1,3,2,0:T(8,128)S(1)}, u32[]{:S(2)}, u32[]{:S(2)}) async-start(f32[128,8,1,2,128]{4,1,3,2,0:T(8,128)} %constant_dynamic-update-slice_fusion), calls=%async_computation | async-start | bytes 2097152 | tf_op jit(solution)/shard_map/all_to_all | solution.py:13
  118.5 0.8 reduce.3
  119.5 3.2 %sort.35 = (s32[256]{0:T(256)}, s32[256]{0:T(256)S(1)}) sort(s32[256]{0:T(256)S(1)} %reshape.23, s32[256]{0:T(256)S(1)} %iota.9), dimensions={0}, to_apply=%region_1.2 | sort | flops 2048 | bytes 4096 | tf_op jit(solution)/shard_map/jit(argsort)/sort | solution.py:74
  122.7 14.2 %all-to-all-done = f32[128,8,1,2,128]{4,1,3,2,0:T(8,128)S(1)} async-done(((f32[128,8,1,2,128]{4,1,3,2,0:T(8,128)}), f32[128,8,1,2,128]{4,1,3,2,0:T(8,128)S(1)}, u32[]{:S(2)}, u32[]{:S(2)}) %all-to-all-start) | async-done | bytes 1048608 | tf_op jit(solution)/shard_map/all_to_all | solution.py:13
  136.8 1.0 gather_fusion.2
  137.9 3.7 %fusion.8 = (f32[256,128]{1,0:T(8,128)S(1)}, f32[27,256,128]{2,0,1:T(8,128)S(1)}) fusion(f32[27,8,1]{0,1,2:T(8,128)S(1)} %copy-done, f32[256,8,128]{2,1,0:T(8,128)S(1)} %gather_fusion.2), kind=kOutput, calls=%fused_computation.294 | convolution fusion | flops 85786624 | bytes 4719456 | tf_op jit(solution)/shard_map/oa,alz->olz/dot_general | solution.py:76
  141.6 0.7 broadcast_divide_fusion
  142.3 3.8 %copy.268 = f32[27,256,128]{2,1,0:T(8,128)} copy(f32[27,256,128]{2,0,1:T(8,128)S(1)} %get-tuple-element.15) | data formatting | bytes 7077888
  (148 shorter events, 76.0 us)
Async XLA Ops:
  1.7 19.4 %collective-permute-start = (f32[16,16,1]{2,1,0:T(8,128)S(1)}, f32[16,16,1]{2,1,0:T(8,128)S(1)}, u32[]{:S(2)}, u32[]{:S(2)}) collective-permute-start(f32[16,16,1]{2,1,0:T(8,128)S(1)} %slice.30), channel_id=1, source_target_pairs={{3,0},{0,1},{1,2},{2,3},{7,4},{4,5},{5,6},{6,7},{11,8},{8,9},{9,10... | collective-permute-start | bytes 3080 | tf_op jit(solution)/shard_map/ppermute | solution.py:20
  10.4 99.1 %all-to-all-start.1 = ((s32[1,128,2]{2,0,1:T(1,128)}), s32[1,128,2]{2,0,1:T(1,128)S(1)}, u32[]{:S(2)}, u32[]{:S(2)}) async-start(s32[1,128,2]{2,0,1:T(1,128)} %bitcast.143), calls=%async_computation.1 | async-start | bytes 131072 | tf_op jit(solution)/shard_map/all_to_all | solution.py:72
  21.2 2.7 %collective-permute-start.1 = (f32[2,1,16,128]{3,2,1,0:T(8,128)S(1)}, f32[2,1,16,128]{3,2,1,0:T(8,128)S(1)}, u32[]{:S(2)}, u32[]{:S(2)}) collective-permute-start(f32[2,1,16,128]{3,2,1,0:T(8,128)S(1)} %fusion.7), channel_id=1, source_target_pairs={{96,0},{0,32},{32,64},{64,96},{97,1},{1,33},{33,65},{65,97},{98,2}... | collective-permute-start | bytes 49160 | tf_op jit(solution)/shard_map/ppermute | solution.py:20
  24.0 6.9 %collective-permute-start.2 = (f32[2,2,16,1,128]{4,3,2,1,0:T(1,128)S(1)}, f32[2,2,16,1,128]{4,3,2,1,0:T(1,128)S(1)}, u32[]{:S(2)}, u32[]{:S(2)}) collective-permute-start(f32[2,2,16,1,128]{4,3,2,1,0:T(1,128)S(1)} %fusion.6), channel_id=1, source_target_pairs={{28,0},{0,4},{4,8},{8,12},{12,16},{16,20},{20,24},{24,28},{29,1},{... | collective-permute-start | bytes 98312 | tf_op jit(solution)/shard_map/ppermute | solution.py:20
  31.7 106.1 %copy-start = (f32[27,8,1]{0,1,2:T(8,128)S(1)}, f32[27,8,1]{0,1,2:T(8,128)}, u32[]{:S(2)}) copy-start(f32[27,8,1]{0,1,2:T(8,128)} %constant.39) | copy-start | bytes 2596
  109.5 27.3 %all-to-all-start = ((f32[128,8,1,2,128]{4,1,3,2,0:T(8,128)}), f32[128,8,1,2,128]{4,1,3,2,0:T(8,128)S(1)}, u32[]{:S(2)}, u32[]{:S(2)}) async-start(f32[128,8,1,2,128]{4,1,3,2,0:T(8,128)} %constant_dynamic-update-slice_fusion), calls=%async_computation | async-start | bytes 2097152 | tf_op jit(solution)/shard_map/all_to_all | solution.py:13
